TPU v7x, 32 devices: a whole 2x2x4 slice. The times are simulated.
32 devices in a mesh: grp: 2 (over y), row: 16 (over z, x, core).
Axes of the slice: x: 2, y: 2, z: 4, core: 2. Of those that a mesh axis runs over, the one named last changes fastest.
Arguments:
- diag_blocks: float32 [8192, 512], P('row'), may hold values from -0.6 to 2.6
- lower_coupling: float32 [8192, 64], P('row'), may hold values from -0.3125 to 0.3125
- upper_coupling: float32 [8192, 64], P('row'), may hold values from -0.3125 to 0.3125
- right_sides: float32 [8192, 1024], P('row', 'grp'), parts along dimension 1, may hold values from -108 to 108
Outputs:
- solution: float32 [8192, 1024], P('row', 'grp'), parts along dimension 1
- res_norms: float32 [8, 1024], P(None, 'grp'), parts along dimension 1
There are 2 independent parts, one for each index of `grp`. A program takes and returns all parts, laid end to end along the dimension named above; an argument that names none is the same for every part. Nothing has to cross between parts.
All inputs are finite; a program needn't handle non-finite values.
Results may differ from a plain program's by a relative error of at most 0.0001.
Values sent between devices are 32-bit elements; how exact they have to be, the bound alone decides.
A program may use at most 64 MiB of HBM per device.

v0:
```python
import jax
import jax.numpy as jnp
from jax import lax
from jax.sharding import PartitionSpec as P

SWEEPS = 8


def extended(shard, sides, width):
    for axis, dim in sides:
        size, length = (lax.axis_size(axis), shard.shape[dim])
        up = [(i, (i + 1) % size) for i in range(size - 1)]
        down = [(j, i) for i, j in up]
        last = lax.slice_in_dim(shard, length - width, length, axis=dim)
        first = lax.slice_in_dim(shard, 0, width, axis=dim)
        before = lax.ppermute(last, axis, up)
        after = lax.ppermute(first, axis, down)
        shard = jnp.concatenate([before, shard, after], axis=dim)
    return shard


def matmul(left, right):
    return jnp.dot(left, right, precision=lax.Precision.HIGHEST, preferred_element_type=jnp.float32)


def local(diag_blocks, lower_coupling, upper_coupling, right_sides):
    pivots = jnp.diagonal(diag_blocks)[:, None]
    width = lower_coupling.shape[1]
    solution = jnp.zeros_like(right_sides)
    partials = []
    for sweep_index in range(SWEEPS):
        padded = extended(solution, (("row", 0),), width)
        before = padded[:width]
        after = padded[padded.shape[0] - width :]
        images = (
            matmul(diag_blocks, solution)
            + matmul(lower_coupling, before)
            + matmul(upper_coupling, after)
        )
        residual = right_sides - images
        local_sums = jnp.sum(residual * residual, axis=0)
        solution = solution + residual / pivots
        partials.append(local_sums)
    res_norms = jnp.sqrt(lax.psum(jnp.stack(partials), "row"))
    return (solution, res_norms)


def solution(mesh):
    return jax.shard_map(
        local,
        mesh=mesh,
        in_specs=(P("row", None), P("row", None), P("row", None), P("row", "grp")),
        out_specs=(P("row", "grp"), P(None, "grp")),
        check_vma=False,
    )
```

profile of v0, /device:TPU:0, one launch (start us, length us, event | category | flops | bytes accessed | tf_op | source)
XLA Modules:
  0.0 163.6 jit_solution(15000186278195526279)
XLA Ops:
  0.7 1.4 collective-permute-start.1
  2.1 3.0 %collective-permute-start = (f32[64,512]{1,0:T(8,128)S(1)}, f32[64,512]{1,0:T(8,128)S(1)}, u32[]{:S(2)}, u32[]{:S(2)}) collective-permute-start(f32[64,512]{1,0:T(8,128)S(1)} %broadcast.16), channel_id=1, source_target_pairs={{0,1},{1,2},{2,3},{3,4},{4,5},{5,6},{6,7},{7,8},{8,9},{9,10},{10,1... | collective-permute-start | bytes 393224 | tf_op jit(solution)/shard_map/ppermute | solution.py:16
  5.2 8.5 %gather_fusion = f32[512]{0:T(512)S(1)} fusion(f32[512,512]{1,0:T(8,128)} %param.4, s32[512]{0:T(512)S(1)} %bitcast.87), kind=kCustom, calls=%fused_computation | custom fusion | bytes 8192 | tf_op jit(solution)/shard_map/jit(diagonal)/cond/branch_0_fun/gather | solution.py:27
  14.9 1.2 multiply_reduce_fusion.7
  16.1 4.5 %collective-permute-start.2 = (f32[64,512]{1,0:T(8,128)S(1)}, f32[64,512]{1,0:T(8,128)S(1)}, u32[]{:S(2)}, u32[]{:S(2)}) collective-permute-start(f32[64,512]{1,0:T(8,128)S(1)} %get-tuple-element.31), channel_id=1, source_target_pairs={{0,1},{1,2},{2,3},{3,4},{4,5},{5,6},{6,7},{7,8},{8,9},{9,10},{10,1... | collective-permute-start | bytes 393224 | tf_op jit(solution)/shard_map/ppermute | solution.py:16
  20.6 1.9 %fusion.25 = f32[512,512]{0,1:T(8,128)S(1)} fusion(f32[512,512]{1,0:T(8,128)S(1)} %get-tuple-element.17, f32[512,512]{1,0:T(8,128)S(1)} %copy-done.1), kind=kOutput, calls=%fused_computation.59 | convolution fusion | flops 1610612736 | bytes 3145728 | tf_op jit(solution)/shard_map/dot_general | solution.py:23
  22.5 1.3 collective-permute-start.3
  25.8 1.2 multiply_reduce_fusion.6
  27.0 5.7 %collective-permute-start.4 = (f32[64,512]{1,0:T(8,128)S(1)}, f32[64,512]{1,0:T(8,128)S(1)}, u32[]{:S(2)}, u32[]{:S(2)}) collective-permute-start(f32[64,512]{1,0:T(8,128)S(1)} %get-tuple-element.29), channel_id=1, source_target_pairs={{0,1},{1,2},{2,3},{3,4},{4,5},{5,6},{6,7},{7,8},{8,9},{9,10},{10,1... | collective-permute-start | bytes 393224 | tf_op jit(solution)/shard_map/ppermute | solution.py:16
  32.7 1.9 %fusion.26 = f32[512,512]{0,1:T(8,128)S(1)} fusion(f32[512,512]{1,0:T(8,128)S(1)} %get-tuple-element.15, f32[512,512]{1,0:T(8,128)S(1)} %copy-done.1), kind=kOutput, calls=%fused_computation.60 | convolution fusion | flops 1610612736 | bytes 3145728 | tf_op jit(solution)/shard_map/dot_general | solution.py:23
  34.6 1.3 collective-permute-start.5
  37.8 1.2 multiply_reduce_fusion.5
  39.0 6.0 %collective-permute-start.6 = (f32[64,512]{1,0:T(8,128)S(1)}, f32[64,512]{1,0:T(8,128)S(1)}, u32[]{:S(2)}, u32[]{:S(2)}) collective-permute-start(f32[64,512]{1,0:T(8,128)S(1)} %get-tuple-element.27), channel_id=1, source_target_pairs={{0,1},{1,2},{2,3},{3,4},{4,5},{5,6},{6,7},{7,8},{8,9},{9,10},{10,1... | collective-permute-start | bytes 393224 | tf_op jit(solution)/shard_map/ppermute | solution.py:16
  45.1 1.9 %fusion.27 = f32[512,512]{0,1:T(8,128)S(1)} fusion(f32[512,512]{1,0:T(8,128)S(1)} %get-tuple-element.13, f32[512,512]{1,0:T(8,128)S(1)} %copy-done.1), kind=kOutput, calls=%fused_computation.61 | convolution fusion | flops 1610612736 | bytes 3145728 | tf_op jit(solution)/shard_map/dot_general | solution.py:23
  47.0 1.3 collective-permute-start.7
  51.4 5.9 %collective-permute-start.8 = (f32[64,512]{1,0:T(8,128)S(1)}, f32[64,512]{1,0:T(8,128)S(1)}, u32[]{:S(2)}, u32[]{:S(2)}) collective-permute-start(f32[64,512]{1,0:T(8,128)S(1)} %get-tuple-element.25), channel_id=1, source_target_pairs={{0,1},{1,2},{2,3},{3,4},{4,5},{5,6},{6,7},{7,8},{8,9},{9,10},{10,1... | collective-permute-start | bytes 393224 | tf_op jit(solution)/shard_map/ppermute | solution.py:16
  57.3 1.9 %fusion.28 = f32[512,512]{0,1:T(8,128)S(1)} fusion(f32[512,512]{1,0:T(8,128)S(1)} %get-tuple-element.11, f32[512,512]{1,0:T(8,128)S(1)} %copy-done.1), kind=kOutput, calls=%fused_computation.62 | convolution fusion | flops 1610612736 | bytes 3145728 | tf_op jit(solution)/shard_map/dot_general | solution.py:23
  59.2 1.3 collective-permute-start.9
  62.4 1.2 multiply_reduce_fusion.3
  63.6 5.9 %collective-permute-start.10 = (f32[64,512]{1,0:T(8,128)S(1)}, f32[64,512]{1,0:T(8,128)S(1)}, u32[]{:S(2)}, u32[]{:S(2)}) collective-permute-start(f32[64,512]{1,0:T(8,128)S(1)} %get-tuple-element.23), channel_id=1, source_target_pairs={{0,1},{1,2},{2,3},{3,4},{4,5},{5,6},{6,7},{7,8},{8,9},{9,10},{10,1... | collective-permute-start | bytes 393224 | tf_op jit(solution)/shard_map/ppermute | solution.py:16
  69.5 1.9 %fusion.29 = f32[512,512]{0,1:T(8,128)S(1)} fusion(f32[512,512]{1,0:T(8,128)S(1)} %get-tuple-element.9, f32[512,512]{1,0:T(8,128)S(1)} %copy-done.1), kind=kOutput, calls=%fused_computation.63 | convolution fusion | flops 1610612736 | bytes 3145728 | tf_op jit(solution)/shard_map/dot_general | solution.py:23
  71.4 1.3 collective-permute-start.11
  74.6 1.2 multiply_reduce_fusion.2
  75.9 6.1 %collective-permute-start.12 = (f32[64,512]{1,0:T(8,128)S(1)}, f32[64,512]{1,0:T(8,128)S(1)}, u32[]{:S(2)}, u32[]{:S(2)}) collective-permute-start(f32[64,512]{1,0:T(8,128)S(1)} %get-tuple-element.21), channel_id=1, source_target_pairs={{0,1},{1,2},{2,3},{3,4},{4,5},{5,6},{6,7},{7,8},{8,9},{9,10},{10,1... | collective-permute-start | bytes 393224 | tf_op jit(solution)/shard_map/ppermute | solution.py:16
  82.0 1.9 %fusion.30 = f32[512,512]{0,1:T(8,128)S(1)} fusion(f32[512,512]{1,0:T(8,128)S(1)} %get-tuple-element.7, f32[512,512]{1,0:T(8,128)S(1)} %copy-done.1), kind=kOutput, calls=%fused_computation.64 | convolution fusion | flops 1610612736 | bytes 3145728 | tf_op jit(solution)/shard_map/dot_general | solution.py:23
  83.8 1.3 collective-permute-start.13
  87.1 1.2 multiply_reduce_fusion.1
  88.3 5.9 %collective-permute-start.14 = (f32[64,512]{1,0:T(8,128)S(1)}, f32[64,512]{1,0:T(8,128)S(1)}, u32[]{:S(2)}, u32[]{:S(2)}) collective-permute-start(f32[64,512]{1,0:T(8,128)S(1)} %get-tuple-element.19), channel_id=1, source_target_pairs={{0,1},{1,2},{2,3},{3,4},{4,5},{5,6},{6,7},{7,8},{8,9},{9,10},{10,1... | collective-permute-start | bytes 393224 | tf_op jit(solution)/shard_map/ppermute | solution.py:16
  94.2 1.9 %fusion.31 = f32[512,512]{0,1:T(8,128)S(1)} fusion(f32[512,512]{1,0:T(8,128)S(1)} %get-tuple-element.5, f32[512,512]{1,0:T(8,128)S(1)} %copy-done.1), kind=kOutput, calls=%fused_computation.65 | convolution fusion | flops 1610612736 | bytes 3145728 | tf_op jit(solution)/shard_map/dot_general | solution.py:23
  96.1 1.3 collective-permute-start.15
  99.3 2.2 %multiply_reduce_fusion = (f32[512]{0:T(512)S(1)}, f32[512,512]{1,0:T(8,128)}) fusion(f32[512,512]{1,0:T(8,128)S(1)} %get-tuple-element.5, f32[512]{0:T(512)S(1)} %gather_fusion, f32[512,512]{1,0:T(8,128)S(1)} %copy-done.3, f32[512,512]{0,1:T(8,128)S(1)} %convolution_add_fusion.1, f32[64,512]{1,0:T(8,128)S(1)} %collective-permute-done.15, ...), kind=kOutput, calls=%fused_computation.33 | convolution fusion | flops 202898944 | bytes 4460544 | tf_op jit(solution)/shard_map/dot_general | solution.py:23
  101.5 61.5 %psum.7 = f32[8,512]{1,0:T(8,128)S(1)} all-reduce(f32[8,512]{1,0:T(8,128)S(1)} %stack.35), channel_id=1, replica_groups=mesh['grp'=2,'row'=16] {'row'}, use_global_device_ids=true, to_apply=%region_9.10 | all-reduce | flops 4096 | bytes 32768 | tf_op jit(solution)/shard_map/psum | solution.py:44
  (45 shorter events, 16.7 us)
Async XLA Ops:
  0.6 13.2 %copy-start = (f32[512,64]{0,1:T(8,128)S(1)}, f32[512,64]{0,1:T(8,128)}, u32[]{:S(2)}) copy-start(f32[512,64]{0,1:T(8,128)} %param.6) | copy-start | bytes 393220
  0.7 13.2 %collective-permute-start.1 = (f32[64,512]{1,0:T(8,128)S(1)}, f32[64,512]{1,0:T(8,128)S(1)}, u32[]{:S(2)}, u32[]{:S(2)}) collective-permute-start(f32[64,512]{1,0:T(8,128)S(1)} %broadcast.16), channel_id=1, source_target_pairs={{1,0},{2,1},{3,2},{4,3},{5,4},{6,5},{7,6},{8,7},{9,8},{10,9},{11,1... | collective-permute-start | bytes 393224 | tf_op jit(solution)/shard_map/ppermute | solution.py:17
  2.1 12.8 %collective-permute-start = (f32[64,512]{1,0:T(8,128)S(1)}, f32[64,512]{1,0:T(8,128)S(1)}, u32[]{:S(2)}, u32[]{:S(2)}) collective-permute-start(f32[64,512]{1,0:T(8,128)S(1)} %broadcast.16), channel_id=1, source_target_pairs={{0,1},{1,2},{2,3},{3,4},{4,5},{5,6},{6,7},{7,8},{8,9},{9,10},{10,1... | collective-permute-start | bytes 393224 | tf_op jit(solution)/shard_map/ppermute | solution.py:16
  5.2 8.5 %copy-start.1 = (f32[512,512]{1,0:T(8,128)S(1)}, f32[512,512]{1,0:T(8,128)}, u32[]{:S(2)}) copy-start(f32[512,512]{1,0:T(8,128)} %param.4) | copy-start | bytes 3145732
  13.6 1.2 copy-start.3
  13.8 1.1 copy-start.2
  16.1 7.7 %collective-permute-start.2 = (f32[64,512]{1,0:T(8,128)S(1)}, f32[64,512]{1,0:T(8,128)S(1)}, u32[]{:S(2)}, u32[]{:S(2)}) collective-permute-start(f32[64,512]{1,0:T(8,128)S(1)} %get-tuple-element.31), channel_id=1, source_target_pairs={{0,1},{1,2},{2,3},{3,4},{4,5},{5,6},{6,7},{7,8},{8,9},{9,10},{10,1... | collective-permute-start | bytes 393224 | tf_op jit(solution)/shard_map/ppermute | solution.py:16
  22.5 3.2 %collective-permute-start.3 = (f32[64,512]{1,0:T(8,128)S(1)}, f32[64,512]{1,0:T(8,128)S(1)}, u32[]{:S(2)}, u32[]{:S(2)}) collective-permute-start(f32[64,512]{1,0:T(8,128)S(1)} %get-tuple-element.30), channel_id=1, source_target_pairs={{1,0},{2,1},{3,2},{4,3},{5,4},{6,5},{7,6},{8,7},{9,8},{10,9},{11,1... | collective-permute-start | bytes 393224 | tf_op jit(solution)/shard_map/ppermute | solution.py:17
  27.0 8.9 %collective-permute-start.4 = (f32[64,512]{1,0:T(8,128)S(1)}, f32[64,512]{1,0:T(8,128)S(1)}, u32[]{:S(2)}, u32[]{:S(2)}) collective-permute-start(f32[64,512]{1,0:T(8,128)S(1)} %get-tuple-element.29), channel_id=1, source_target_pairs={{0,1},{1,2},{2,3},{3,4},{4,5},{5,6},{6,7},{7,8},{8,9},{9,10},{10,1... | collective-permute-start | bytes 393224 | tf_op jit(solution)/shard_map/ppermute | solution.py:16
  34.6 3.2 %collective-permute-start.5 = (f32[64,512]{1,0:T(8,128)S(1)}, f32[64,512]{1,0:T(8,128)S(1)}, u32[]{:S(2)}, u32[]{:S(2)}) collective-permute-start(f32[64,512]{1,0:T(8,128)S(1)} %get-tuple-element.28), channel_id=1, source_target_pairs={{1,0},{2,1},{3,2},{4,3},{5,4},{6,5},{7,6},{8,7},{9,8},{10,9},{11,1... | collective-permute-start | bytes 393224 | tf_op jit(solution)/shard_map/ppermute | solution.py:17
  39.0 9.2 %collective-permute-start.6 = (f32[64,512]{1,0:T(8,128)S(1)}, f32[64,512]{1,0:T(8,128)S(1)}, u32[]{:S(2)}, u32[]{:S(2)}) collective-permute-start(f32[64,512]{1,0:T(8,128)S(1)} %get-tuple-element.27), channel_id=1, source_target_pairs={{0,1},{1,2},{2,3},{3,4},{4,5},{5,6},{6,7},{7,8},{8,9},{9,10},{10,1... | collective-permute-start | bytes 393224 | tf_op jit(solution)/shard_map/ppermute | solution.py:16
  47.0 3.2 %collective-permute-start.7 = (f32[64,512]{1,0:T(8,128)S(1)}, f32[64,512]{1,0:T(8,128)S(1)}, u32[]{:S(2)}, u32[]{:S(2)}) collective-permute-start(f32[64,512]{1,0:T(8,128)S(1)} %get-tuple-element.26), channel_id=1, source_target_pairs={{1,0},{2,1},{3,2},{4,3},{5,4},{6,5},{7,6},{8,7},{9,8},{10,9},{11,1... | collective-permute-start | bytes 393224 | tf_op jit(solution)/shard_map/ppermute | solution.py:17
  51.4 9.1 %collective-permute-start.8 = (f32[64,512]{1,0:T(8,128)S(1)}, f32[64,512]{1,0:T(8,128)S(1)}, u32[]{:S(2)}, u32[]{:S(2)}) collective-permute-start(f32[64,512]{1,0:T(8,128)S(1)} %get-tuple-element.25), channel_id=1, source_target_pairs={{0,1},{1,2},{2,3},{3,4},{4,5},{5,6},{6,7},{7,8},{8,9},{9,10},{10,1... | collective-permute-start | bytes 393224 | tf_op jit(solution)/shard_map/ppermute | solution.py:16
  59.2 3.2 %collective-permute-start.9 = (f32[64,512]{1,0:T(8,128)S(1)}, f32[64,512]{1,0:T(8,128)S(1)}, u32[]{:S(2)}, u32[]{:S(2)}) collective-permute-start(f32[64,512]{1,0:T(8,128)S(1)} %get-tuple-element.24), channel_id=1, source_target_pairs={{1,0},{2,1},{3,2},{4,3},{5,4},{6,5},{7,6},{8,7},{9,8},{10,9},{11,1... | collective-permute-start | bytes 393224 | tf_op jit(solution)/shard_map/ppermute | solution.py:17
  63.6 9.1 %collective-permute-start.10 = (f32[64,512]{1,0:T(8,128)S(1)}, f32[64,512]{1,0:T(8,128)S(1)}, u32[]{:S(2)}, u32[]{:S(2)}) collective-permute-start(f32[64,512]{1,0:T(8,128)S(1)} %get-tuple-element.23), channel_id=1, source_target_pairs={{0,1},{1,2},{2,3},{3,4},{4,5},{5,6},{6,7},{7,8},{8,9},{9,10},{10,1... | collective-permute-start | bytes 393224 | tf_op jit(solution)/shard_map/ppermute | solution.py:16
  71.4 3.2 %collective-permute-start.11 = (f32[64,512]{1,0:T(8,128)S(1)}, f32[64,512]{1,0:T(8,128)S(1)}, u32[]{:S(2)}, u32[]{:S(2)}) collective-permute-start(f32[64,512]{1,0:T(8,128)S(1)} %get-tuple-element.22), channel_id=1, source_target_pairs={{1,0},{2,1},{3,2},{4,3},{5,4},{6,5},{7,6},{8,7},{9,8},{10,9},{11,1... | collective-permute-start | bytes 393224 | tf_op jit(solution)/shard_map/ppermute | solution.py:17
  75.9 9.3 %collective-permute-start.12 = (f32[64,512]{1,0:T(8,128)S(1)}, f32[64,512]{1,0:T(8,128)S(1)}, u32[]{:S(2)}, u32[]{:S(2)}) collective-permute-start(f32[64,512]{1,0:T(8,128)S(1)} %get-tuple-element.21), channel_id=1, source_target_pairs={{0,1},{1,2},{2,3},{3,4},{4,5},{5,6},{6,7},{7,8},{8,9},{9,10},{10,1... | collective-permute-start | bytes 393224 | tf_op jit(solution)/shard_map/ppermute | solution.py:16
  83.8 3.2 %collective-permute-start.13 = (f32[64,512]{1,0:T(8,128)S(1)}, f32[64,512]{1,0:T(8,128)S(1)}, u32[]{:S(2)}, u32[]{:S(2)}) collective-permute-start(f32[64,512]{1,0:T(8,128)S(1)} %get-tuple-element.20), channel_id=1, source_target_pairs={{1,0},{2,1},{3,2},{4,3},{5,4},{6,5},{7,6},{8,7},{9,8},{10,9},{11,1... | collective-permute-start | bytes 393224 | tf_op jit(solution)/shard_map/ppermute | solution.py:17
  88.3 9.1 %collective-permute-start.14 = (f32[64,512]{1,0:T(8,128)S(1)}, f32[64,512]{1,0:T(8,128)S(1)}, u32[]{:S(2)}, u32[]{:S(2)}) collective-permute-start(f32[64,512]{1,0:T(8,128)S(1)} %get-tuple-element.19), channel_id=1, source_target_pairs={{0,1},{1,2},{2,3},{3,4},{4,5},{5,6},{6,7},{7,8},{8,9},{9,10},{10,1... | collective-permute-start | bytes 393224 | tf_op jit(solution)/shard_map/ppermute | solution.py:16
  96.1 3.2 %collective-permute-start.15 = (f32[64,512]{1,0:T(8,128)S(1)}, f32[64,512]{1,0:T(8,128)S(1)}, u32[]{:S(2)}, u32[]{:S(2)}) collective-permute-start(f32[64,512]{1,0:T(8,128)S(1)} %get-tuple-element.18), channel_id=1, source_target_pairs={{1,0},{2,1},{3,2},{4,3},{5,4},{6,5},{7,6},{8,7},{9,8},{10,9},{11,1... | collective-permute-start | bytes 393224 | tf_op jit(solution)/shard_map/ppermute | solution.py:17
where the time goes:
time: 164 us
  blocking collectives  61.5 us (38%)
  starting transfers between devices  53.4 us (33%)
  matrix products  31.8 us (19%)
  local copies, waits for them, and re-layouts  9.29 us (6%)
  waiting for transfers between devices  6.33 us (4%)
    psum x1, blocking collectives, local(): res_norms = jnp.sqrt(lax.psum(jnp.stack(partials), 'row'))  61.5 us
    ppermute x8, starting transfers between devices, extended(): before = lax.ppermute(last, axis, up)  42.9 us
    dot_general x23, matrix products, matmul(): jnp.dot(left, right, precision=lax.Precision.HIGHEST, preferred_element_t...  31.8 us
    ppermute x8, starting transfers between devices, extended(): after = lax.ppermute(first, axis, down)  10.5 us
    gather x1, local copies, waits for them, and re-layouts, local(): pivots = jnp.diagonal(diag_blocks)[:, None]  8.46 us
    ppermute x8, waiting for transfers between devices, extended(): after = lax.ppermute(first, axis, down)  6.31 us
  transfers between devices with their start and end apart: 16, of which 7 were waited for; matrix products, arithmetic and copies ran while one was open for 18% of the time, Pallas kernels for 0%

commit v1 on v0

v1 whole, which is shorter than its diff:
```python
import functools

import jax
import jax.numpy as jnp
from jax import lax
from jax.experimental import pallas as pl
from jax.experimental.pallas import tpu as pltpu
from jax.sharding import PartitionSpec as P

SWEEPS = 8
LANES = 128


def split(value):
    high = value.astype(jnp.bfloat16)
    low = (value - high.astype(jnp.float32)).astype(jnp.bfloat16)
    return high, low


def dot(left, right):
    return jnp.dot(left, right, preferred_element_type=jnp.float32)


def kernel(
    n, d_hbm, l_hbm, u_hbm, b_hbm, x_out, norm_out,
    dv, lv, uv, xs, a_hi, a_lo, c_hi, c_lo, inv, acc, rhs, halo,
    send, recv, part, parts, load_sem, send_sem, recv_sem, psend, precv, out_sem,
):
    me = lax.axis_index("row")
    rows, cols = xs.shape
    width = lv.shape[1]
    groups = cols // LANES
    has = (me > 0, me < n - 1)
    last = rows - width

    loads = [pltpu.make_async_copy(d_hbm, dv, load_sem.at[0]),
             pltpu.make_async_copy(b_hbm, xs, load_sem.at[1]),
             pltpu.make_async_copy(l_hbm, lv, load_sem.at[2]),
             pltpu.make_async_copy(u_hbm, uv, load_sem.at[3])]
    for load in loads:
        load.start()

    barrier = pltpu.get_barrier_semaphore()

    def greet(o, carry):
        pl.semaphore_signal(barrier, inc=1, device_id={"row": lax.rem(me + o, n)})
        return carry

    lax.fori_loop(1, n, greet, 0)

    for side in range(2):
        @pl.when(jnp.logical_not(has[side]))
        def _():
            recv[:, side] = jnp.zeros_like(recv[:, side])

    def copy(s, side, g):
        target = me + 1 if side == 0 else me - 1
        return pltpu.make_async_remote_copy(
            src_ref=send.at[s, side, g], dst_ref=recv.at[s, side, g],
            send_sem=send_sem.at[s, side, g], recv_sem=recv_sem.at[s, side, g],
            device_id={"row": target})

    def ship(s, g):
        for side in range(2):
            @pl.when(has[1 - side])
            def _():
                copy(s, side, g).start()

    def keep(r, top, g):
        size = r.shape[0]
        d = r * inv[top:top + size]
        high, low = split(d)
        rhs[top:top + size, :LANES] = high
        rhs[top:top + size, LANES:] = low
        return d, jnp.sum(r * r, axis=0, keepdims=True)

    def advance(g):
        both = dot(a_hi[...], rhs[...])
        acc[g] = both[:, :LANES] + both[:, LANES:] + dot(a_lo[...], rhs[:, :LANES])

    def span(g):
        return slice(g * LANES, (g + 1) * LANES)

    loads[0].wait()
    for m in range(rows // LANES):
        block = dv[m * LANES:(m + 1) * LANES, m * LANES:(m + 1) * LANES]
        eye = (lax.broadcasted_iota(jnp.int32, block.shape, 0)
               == lax.broadcasted_iota(jnp.int32, block.shape, 1))
        pivot = jnp.sum(jnp.where(eye, block, 0.0), axis=1, keepdims=True)
        inv[m * LANES:(m + 1) * LANES] = jnp.broadcast_to(1.0 / pivot, block.shape)
    loads[1].wait()
    for g in range(groups):
        send[0, 1, g] = xs[:width, span(g)] * inv[:width]
        send[0, 0, g] = xs[last:, span(g)] * inv[last:]
    pl.semaphore_wait(barrier, n - 1)
    for g in range(groups):
        ship(0, g)

    for m in range(rows // LANES):
        block = dv[m * LANES:(m + 1) * LANES]
        eye = (lax.broadcasted_iota(jnp.int32, block.shape, 0) + m * LANES
               == lax.broadcasted_iota(jnp.int32, block.shape, 1))
        a_hi[m * LANES:(m + 1) * LANES], a_lo[m * LANES:(m + 1) * LANES] = split(
            jnp.where(eye, 0.0, -block))
    loads[2].wait()
    loads[3].wait()
    c_hi[...], c_lo[...] = split(-jnp.concatenate([lv[...], uv[...]], axis=1))

    for g in range(groups):
        d, sums = keep(xs[:, span(g)], 0, g)
        part[0, g:g + 1] = sums
        xs[:, span(g)] = d
        advance(g)

    def sweep(s, final):
        for g in range(groups):
            for side in range(2):
                @pl.when(has[side])
                def _():
                    copy(s - 1, side, g).wait_recv()
            for side in range(2):
                high, low = split(recv[s - 1, side, g])
                halo[side * width:(side + 1) * width, :LANES] = high
                halo[side * width:(side + 1) * width, LANES:] = low

            def rest(top, size):
                both = dot(c_hi[top:top + size], halo[...])
                cross = dot(c_lo[top:top + size], halo[:, :LANES])
                return acc[g, top:top + size] + (both[:, :LANES] + both[:, LANES:] + cross)

            total = jnp.zeros((1, LANES), jnp.float32)
            for top, size in ((0, width), (last, width), (width, last - width)):
                d, sums = keep(rest(top, size), top, g)
                total = total + sums
                if size == width and not final:
                    send[s, 1 if top == 0 else 0, g] = d
                    if top == last:
                        ship(s, g)
                xs[top:top + size, span(g)] += d
            part[s, g:g + 1] = total
            if final:
                pltpu.make_async_copy(
                    xs.at[:, span(g)], x_out.at[:, span(g)], out_sem.at[g]).start()
            else:
                advance(g)

    def body(s, carry):
        sweep(s, False)
        return carry

    def spread(lane, start):
        lo, hi = ((0, SWEEPS - 1), (SWEEPS - 1, SWEEPS))[lane]

        def one(o, carry):
            peer = pltpu.make_async_remote_copy(
                src_ref=part.at[lo:hi], dst_ref=parts.at[me, lo:hi],
                send_sem=psend.at[lane, o], recv_sem=precv.at[lane, o],
                device_id={"row": lax.rem(me + o, n)})
            if start:
                peer.start()
            else:
                peer.wait_send()
            return carry

        lax.fori_loop(1, n, one, 0)

    def collect(lane):
        lo, hi = ((0, SWEEPS - 1), (SWEEPS - 1, SWEEPS))[lane]

        def one(o, carry):
            source = lax.rem(me + n - o, n)
            pltpu.make_async_remote_copy(
                src_ref=part.at[lo:hi], dst_ref=parts.at[source, lo:hi],
                send_sem=psend.at[lane, o], recv_sem=precv.at[lane, o],
                device_id={"row": lax.rem(me + o, n)}).wait_recv()
            return carry

        lax.fori_loop(1, n, one, 0)

    lax.fori_loop(1, SWEEPS - 1, body, 0)
    spread(0, True)
    sweep(SWEEPS - 1, True)
    spread(1, True)
    parts[me] = part[...]

    def drain(s, carry):
        for side in range(2):
            for g in range(groups):
                @pl.when(has[1 - side])
                def _():
                    copy(s, side, g).wait_send()
        return carry

    lax.fori_loop(0, SWEEPS - 1, drain, 0)
    collect(0)
    collect(1)
    norms = jnp.sqrt(lax.fori_loop(0, n, lambda j, t: t + parts[j], jnp.zeros(part.shape, jnp.float32)))
    for s in range(SWEEPS):
        for g in range(groups):
            norm_out[s:s + 1, span(g)] = norms[s, g:g + 1]
    spread(0, False)
    spread(1, False)
    for g in range(groups):
        pltpu.make_async_copy(xs.at[:, span(g)], x_out.at[:, span(g)], out_sem.at[g]).wait()


def local(n, diag_blocks, lower_coupling, upper_coupling, right_sides):
    rows, cols = right_sides.shape
    width = lower_coupling.shape[1]
    groups = cols // LANES
    f32, bf16 = jnp.float32, jnp.bfloat16
    return pl.pallas_call(
        functools.partial(kernel, n),
        out_shape=(jax.ShapeDtypeStruct((rows, cols), f32), jax.ShapeDtypeStruct((SWEEPS, cols), f32)),
        in_specs=[pl.BlockSpec(memory_space=pl.ANY)] * 4,
        out_specs=(pl.BlockSpec(memory_space=pl.ANY), pl.BlockSpec(memory_space=pltpu.VMEM)),
        scratch_shapes=[
            pltpu.VMEM((rows, rows), f32),
            pltpu.VMEM((rows, width), f32),
            pltpu.VMEM((rows, width), f32),
            pltpu.VMEM((rows, cols), f32),
            pltpu.VMEM((rows, rows), bf16),
            pltpu.VMEM((rows, rows), bf16),
            pltpu.VMEM((rows, 2 * width), bf16),
            pltpu.VMEM((rows, 2 * width), bf16),
            pltpu.VMEM((rows, LANES), f32),
            pltpu.VMEM((groups, rows, LANES), f32),
            pltpu.VMEM((rows, 2 * LANES), bf16),
            pltpu.VMEM((2 * width, 2 * LANES), bf16),
            pltpu.VMEM((SWEEPS - 1, 2, groups, width, LANES), f32),
            pltpu.VMEM((SWEEPS - 1, 2, groups, width, LANES), f32),
            pltpu.VMEM((SWEEPS, groups, LANES), f32),
            pltpu.VMEM((n, SWEEPS, groups, LANES), f32),
            pltpu.SemaphoreType.DMA((4,)),
            pltpu.SemaphoreType.DMA((SWEEPS - 1, 2, groups)),
            pltpu.SemaphoreType.DMA((SWEEPS - 1, 2, groups)),
            pltpu.SemaphoreType.DMA((2, n)),
            pltpu.SemaphoreType.DMA((2, n)),
            pltpu.SemaphoreType.DMA((groups,)),
        ],
        compiler_params=pltpu.CompilerParams(collective_id=0, has_side_effects=True),
    )(diag_blocks, lower_coupling, upper_coupling, right_sides)


def solution(mesh):
    return jax.shard_map(
        functools.partial(local, mesh.shape["row"]),
        mesh=mesh,
        in_specs=(P("row", None), P("row", None), P("row", None), P("row", "grp")),
        out_specs=(P("row", "grp"), P(None, "grp")),
        check_vma=False,
    )
```

time: 164 us -> 45.7 us (0.28)
  blocking collectives: 61.5 us -> 0 us
  starting transfers between devices: 53.4 us -> 0 us
  Pallas kernels: 0 us -> 39.3 us
  matrix products: 31.8 us -> 0 us
  waiting for transfers between devices: 6.33 us -> 0 us
  local copies, waits for them, and re-layouts: 9.29 us -> 5.49 us
    psum x1 -> x0, blocking collectives: 61.5 us -> none  [local(): res_norms = jnp.sqrt(lax.psum(jnp.stack(partials), 'row'))]
    ppermute x16 -> x0, starting transfers between devices: 53.4 us -> none  [the longest x8 42.9 us: extended(): before = lax.ppermute(last, axis, up)]
    pallas_call x0 -> x1, Pallas kernels: none -> 39.3 us  [local(): pl.pallas_call(functools.partial(kernel, n), out_shape=(jax.ShapeDtypeStr...]
    dot_general x23 -> x0, matrix products: 31.8 us -> none  [matmul(): jnp.dot(left, right, precision=lax.Precision.HIGHEST, preferred_element_t...]
    gather x1 -> x0, local copies, waits for them, and re-layouts: 8.46 us -> none  [local(): pivots = jnp.diagonal(diag_blocks)[:, None]]
    ppermute x16 -> x0, waiting for transfers between devices: 6.33 us -> none  [the longest x8 6.31 us: extended(): after = lax.ppermute(first, axis, down)]
    unnamed x8, local copies, waits for them, and re-layouts: 0.03 us -> 5.49 us
  transfers between devices with their start and end apart: 16 -> 0, of which waited for: 7 -> 0; matrix products, arithmetic and copies ran while one was open for 18% -> 0% of each run, Pallas kernels for 0% -> 0%
where the time goes in v1:
time: 45.7 us; the launch traced here: 45.5 us
  Pallas kernels  39.3 us (86%)
  local copies, waits for them, and re-layouts  5.49 us (12%)
  between operations  0.66 us (1%)
    pallas_call x1, Pallas kernels, local(): pl.pallas_call(functools.partial(kernel, n), out_shape=(jax.ShapeDtypeStr...  39.3 us
    unnamed x8, local copies, waits for them, and re-layouts  5.49 us

profile of v1, /device:TPU:0, one launch (start us, length us, event | category | flops | bytes accessed | tf_op | source)
XLA Modules:
  0.0 45.5 jit_solution(5389700080909375860)
XLA Ops:
  0.6 0.0 copy-start
  0.6 1.8 %copy.6.l_hbm = f32[512,64]{1,0:T(8,128)} copy(f32[512,64]{0,1:T(8,128)} %param.5) | data formatting | bytes 262144 | tf_op args[1]
  2.4 0.0 copy-done
  2.4 0.8 %copy.7.u_hbm = f32[512,64]{1,0:T(8,128)} copy(f32[512,64]{0,1:T(8,128)S(1)} %copy-done) | data formatting | bytes 262144 | tf_op args[2]
  3.3 39.3 %shard_map.59 = (f32[512,512]{1,0:T(8,128)}, f32[8,512]{1,0:T(8,128)}) custom-call(f32[512,512]{1,0:T(8,128)} %d_hbm.1, f32[512,64]{1,0:T(8,128)} %copy.6.l_hbm, f32[512,64]{1,0:T(8,128)} %copy.7.u_hbm, f32[512,512]{1,0:T(8,128)} %b_hbm.1), custom_call_target="tpu_custom_call" | custom-call | tf_op jit(solution)/shard_map/pallas_call | solution.py:212
  42.6 0.0 copy-start.1
  42.6 2.3 %copy.10 = f32[512,512]{1,0:T(8,128)} copy(f32[512,512]{1,0:T(8,128)} %get-tuple-element.4) | data formatting | bytes 2097152
  44.9 0.0 copy-done.1
  44.9 0.6 %copy.11 = f32[8,512]{1,0:T(8,128)} copy(f32[8,512]{1,0:T(8,128)S(1)} %copy-done.1) | data formatting | bytes 32768
Async XLA Ops:
  0.6 1.8 %copy-start = (f32[512,64]{0,1:T(8,128)S(1)}, f32[512,64]{0,1:T(8,128)}, u32[]{:S(2)}) copy-start(f32[512,64]{0,1:T(8,128)} %param.6) | copy-start | bytes 393220
  42.6 2.3 %copy-start.1 = (f32[8,512]{1,0:T(8,128)S(1)}, f32[8,512]{1,0:T(8,128)}, u32[]{:S(2)}) copy-start(f32[8,512]{1,0:T(8,128)} %get-tuple-element.5) | copy-start | bytes 49156

commit v2 on v1

--- a/solution.py
+++ b/solution.py
@@ -24,11 +24,11 @@
 def kernel(
     n, d_hbm, l_hbm, u_hbm, b_hbm, x_out, norm_out,
     dv, lv, uv, xs, a_hi, a_lo, c_hi, c_lo, inv, acc, rhs, halo,
-    send, recv, part, parts, load_sem, send_sem, recv_sem, psend, precv, out_sem,
+    send, recv, part, nears, fars, lates, load_sem, send_sem, recv_sem, psend, precv, out_sem,
 ):
     me = lax.axis_index("row")
     rows, cols = xs.shape
-    width = lv.shape[1]
+    width = lv.shape[0]
     groups = cols // LANES
     has = (me > 0, me < n - 1)
     last = rows - width
@@ -104,7 +104,7 @@
             jnp.where(eye, 0.0, -block))
     loads[2].wait()
     loads[3].wait()
-    c_hi[...], c_lo[...] = split(-jnp.concatenate([lv[...], uv[...]], axis=1))
+    c_hi[...], c_lo[...] = split(-jnp.concatenate([lv[...], uv[...]], axis=0).T)
 
     for g in range(groups):
         d, sums = keep(xs[:, span(g)], 0, g)
@@ -148,40 +148,48 @@
         sweep(s, False)
         return carry
 
-    def spread(lane, start):
-        lo, hi = ((0, SWEEPS - 1), (SWEEPS - 1, SWEEPS))[lane]
-
+    inner = nears.shape[0]
+    outer = n // inner
+    seat, bench = lax.rem(me, inner), lax.div(me, inner)
+    done = SWEEPS - 1
+
+    def near(o):
+        return pltpu.make_async_remote_copy(
+            src_ref=part.at[:done], dst_ref=nears.at[seat],
+            send_sem=psend.at[0, o], recv_sem=precv.at[0, o],
+            device_id={"row": bench * inner + lax.rem(seat + o, inner)})
+
+    def far(o):
+        return pltpu.make_async_remote_copy(
+            src_ref=fars.at[bench], dst_ref=fars.at[bench],
+            send_sem=psend.at[1, o], recv_sem=precv.at[1, o],
+            device_id={"row": lax.rem(bench + o, outer) * inner + seat})
+
+    def late(o):
+        return pltpu.make_async_remote_copy(
+            src_ref=part.at[done], dst_ref=lates.at[me],
+            send_sem=psend.at[2, o], recv_sem=precv.at[2, o],
+            device_id={"row": lax.rem(me + o, n)})
+
+    def over(count, action):
         def one(o, carry):
-            peer = pltpu.make_async_remote_copy(
-                src_ref=part.at[lo:hi], dst_ref=parts.at[me, lo:hi],
-                send_sem=psend.at[lane, o], recv_sem=precv.at[lane, o],
-                device_id={"row": lax.rem(me + o, n)})
-            if start:
-                peer.start()
-            else:
-                peer.wait_send()
+            action(o)
             return carry
 
-        lax.fori_loop(1, n, one, 0)
-
-    def collect(lane):
-        lo, hi = ((0, SWEEPS - 1), (SWEEPS - 1, SWEEPS))[lane]
-
-        def one(o, carry):
-            source = lax.rem(me + n - o, n)
-            pltpu.make_async_remote_copy(
-                src_ref=part.at[lo:hi], dst_ref=parts.at[source, lo:hi],
-                send_sem=psend.at[lane, o], recv_sem=precv.at[lane, o],
-                device_id={"row": lax.rem(me + o, n)}).wait_recv()
-            return carry
-
-        lax.fori_loop(1, n, one, 0)
+        lax.fori_loop(1, count, one, 0)
 
     lax.fori_loop(1, SWEEPS - 1, body, 0)
-    spread(0, True)
+    over(inner, lambda o: near(o).start())
+    nears[seat] = part[:done]
     sweep(SWEEPS - 1, True)
-    spread(1, True)
-    parts[me] = part[...]
+    over(n, lambda o: late(o).start())
+    lates[me] = part[done]
+    over(inner, lambda o: near(o).wait_recv())
+    sums = nears[0]
+    for j in range(1, inner):
+        sums = sums + nears[j]
+    fars[bench] = sums
+    over(outer, lambda o: far(o).start())
 
     def drain(s, carry):
         for side in range(2):
@@ -192,14 +200,21 @@
         return carry
 
     lax.fori_loop(0, SWEEPS - 1, drain, 0)
-    collect(0)
-    collect(1)
-    norms = jnp.sqrt(lax.fori_loop(0, n, lambda j, t: t + parts[j], jnp.zeros(part.shape, jnp.float32)))
-    for s in range(SWEEPS):
+    over(inner, lambda o: near(o).wait_send())
+    over(outer, lambda o: far(o).wait_recv())
+    norms = fars[0]
+    for j in range(1, outer):
+        norms = norms + fars[j]
+    norms = jnp.sqrt(norms)
+    for s in range(done):
         for g in range(groups):
             norm_out[s:s + 1, span(g)] = norms[s, g:g + 1]
-    spread(0, False)
-    spread(1, False)
+    over(n, lambda o: late(o).wait_recv())
+    norm = jnp.sqrt(lax.fori_loop(1, n, lambda j, t: t + lates[j], lates[0]))
+    for g in range(groups):
+        norm_out[done:, span(g)] = norm[g:g + 1]
+    over(outer, lambda o: far(o).wait_send())
+    over(n, lambda o: late(o).wait_send())
     for g in range(groups):
         pltpu.make_async_copy(xs.at[:, span(g)], x_out.at[:, span(g)], out_sem.at[g]).wait()
 
@@ -208,6 +223,7 @@
     rows, cols = right_sides.shape
     width = lower_coupling.shape[1]
     groups = cols // LANES
+    inner = max(a for a in range(1, n + 1) if n % a == 0 and a * a <= n)
     f32, bf16 = jnp.float32, jnp.bfloat16
     return pl.pallas_call(
         functools.partial(kernel, n),
@@ -216,8 +232,8 @@
         out_specs=(pl.BlockSpec(memory_space=pl.ANY), pl.BlockSpec(memory_space=pltpu.VMEM)),
         scratch_shapes=[
             pltpu.VMEM((rows, rows), f32),
-            pltpu.VMEM((rows, width), f32),
-            pltpu.VMEM((rows, width), f32),
+            pltpu.VMEM((width, rows), f32),
+            pltpu.VMEM((width, rows), f32),
             pltpu.VMEM((rows, cols), f32),
             pltpu.VMEM((rows, rows), bf16),
             pltpu.VMEM((rows, rows), bf16),
@@ -230,16 +246,19 @@
             pltpu.VMEM((SWEEPS - 1, 2, groups, width, LANES), f32),
             pltpu.VMEM((SWEEPS - 1, 2, groups, width, LANES), f32),
             pltpu.VMEM((SWEEPS, groups, LANES), f32),
-            pltpu.VMEM((n, SWEEPS, groups, LANES), f32),
+            pltpu.VMEM((inner, SWEEPS - 1, groups, LANES), f32),
+            pltpu.VMEM((n // inner, SWEEPS - 1, groups, LANES), f32),
+            pltpu.VMEM((n, groups, LANES), f32),
             pltpu.SemaphoreType.DMA((4,)),
             pltpu.SemaphoreType.DMA((SWEEPS - 1, 2, groups)),
             pltpu.SemaphoreType.DMA((SWEEPS - 1, 2, groups)),
-            pltpu.SemaphoreType.DMA((2, n)),
-            pltpu.SemaphoreType.DMA((2, n)),
+            pltpu.SemaphoreType.DMA((3, n)),
+            pltpu.SemaphoreType.DMA((3, n)),
             pltpu.SemaphoreType.DMA((groups,)),
         ],
-        compiler_params=pltpu.CompilerParams(collective_id=0, has_side_effects=True),
-    )(diag_blocks, lower_coupling, upper_coupling, right_sides)
+        compiler_params=pltpu.CompilerParams(
+            collective_id=0, has_side_effects=True),
+    )(diag_blocks, lower_coupling.T, upper_coupling.T, right_sides)
 
 
 def solution(mesh):

time: 45.7 us -> 42.4 us (0.928)
  local copies, waits for them, and re-layouts: 5.49 us -> 2.88 us
  Pallas kernels: 39.3 us -> 38.7 us
    unnamed x8 -> x4, local copies, waits for them, and re-layouts: 5.49 us -> 2.88 us
    pallas_call x1, Pallas kernels: 39.3 us -> 38.7 us  [local(): pl.pallas_call(functools.partial(kernel, n), out_shape=(jax.ShapeDtypeStr...]
where the time goes in v2:
time: 42.4 us; the launch traced here: 42.2 us
  Pallas kernels  38.7 us (91%)
  local copies, waits for them, and re-layouts  2.88 us (7%)
  between operations  0.65 us (2%)
    pallas_call x1, Pallas kernels, local(): pl.pallas_call(functools.partial(kernel, n), out_shape=(jax.ShapeDtypeStr...  38.7 us
    unnamed x4, local copies, waits for them, and re-layouts  2.88 us

profile of v2, /device:TPU:0, one launch (start us, length us, event | category | flops | bytes accessed | tf_op | source)
XLA Modules:
  0.0 42.2 jit_solution(15200056917069258952)
XLA Ops:
  0.6 38.7 %shard_map.59 = (f32[512,512]{1,0:T(8,128)}, f32[8,512]{1,0:T(8,128)}) custom-call(f32[512,512]{1,0:T(8,128)} %d_hbm.1, f32[64,512]{1,0:T(8,128)} %bitcast.2, f32[64,512]{1,0:T(8,128)} %bitcast.3, f32[512,512]{1,0:T(8,128)} %b_hbm.1), custom_call_target="tpu_custom_call" | custom-call | tf_op jit(solution)/shard_map/pallas_call | solution.py:228
  39.3 0.0 copy-start
  39.3 2.3 %copy.8 = f32[512,512]{1,0:T(8,128)} copy(f32[512,512]{1,0:T(8,128)} %get-tuple-element.4) | data formatting | bytes 2097152
  41.6 0.0 copy-done
  41.6 0.6 %copy.9 = f32[8,512]{1,0:T(8,128)} copy(f32[8,512]{1,0:T(8,128)S(1)} %copy-done) | data formatting | bytes 32768
Async XLA Ops:
  39.3 2.3 %copy-start = (f32[8,512]{1,0:T(8,128)S(1)}, f32[8,512]{1,0:T(8,128)}, u32[]{:S(2)}) copy-start(f32[8,512]{1,0:T(8,128)} %get-tuple-element.5) | copy-start | bytes 49156

commit v3 on v2

--- a/solution.py
+++ b/solution.py
@@ -24,7 +24,7 @@
 def kernel(
     n, d_hbm, l_hbm, u_hbm, b_hbm, x_out, norm_out,
     dv, lv, uv, xs, a_hi, a_lo, c_hi, c_lo, inv, acc, rhs, halo,
-    send, recv, part, nears, fars, lates, load_sem, send_sem, recv_sem, psend, precv, out_sem,
+    send, recv, part, nears, fars, lates, load_sem, send_sem, recv_sem, psend, precv,
 ):
     me = lax.axis_index("row")
     rows, cols = xs.shape
@@ -136,12 +136,12 @@
                     send[s, 1 if top == 0 else 0, g] = d
                     if top == last:
                         ship(s, g)
-                xs[top:top + size, span(g)] += d
+                if final:
+                    x_out[top:top + size, span(g)] = xs[top:top + size, span(g)] + d
+                else:
+                    xs[top:top + size, span(g)] += d
             part[s, g:g + 1] = total
-            if final:
-                pltpu.make_async_copy(
-                    xs.at[:, span(g)], x_out.at[:, span(g)], out_sem.at[g]).start()
-            else:
+            if not final:
                 advance(g)
 
     def body(s, carry):
@@ -215,8 +215,6 @@
         norm_out[done:, span(g)] = norm[g:g + 1]
     over(outer, lambda o: far(o).wait_send())
     over(n, lambda o: late(o).wait_send())
-    for g in range(groups):
-        pltpu.make_async_copy(xs.at[:, span(g)], x_out.at[:, span(g)], out_sem.at[g]).wait()
 
 
 def local(n, diag_blocks, lower_coupling, upper_coupling, right_sides):
@@ -227,9 +225,9 @@
     f32, bf16 = jnp.float32, jnp.bfloat16
     return pl.pallas_call(
         functools.partial(kernel, n),
-        out_shape=(jax.ShapeDtypeStruct((rows, cols), f32), jax.ShapeDtypeStruct((SWEEPS, cols), f32)),
-        in_specs=[pl.BlockSpec(memory_space=pl.ANY)] * 4,
-        out_specs=(pl.BlockSpec(memory_space=pl.ANY), pl.BlockSpec(memory_space=pltpu.VMEM)),
+        out_shape=(pltpu.VMEM((rows, cols), f32), pltpu.VMEM((SWEEPS, cols), f32)),
+        in_specs=[pl.BlockSpec(memory_space=pltpu.HBM)] * 4,
+        out_specs=[pl.BlockSpec(memory_space=pltpu.VMEM)] * 2,
         scratch_shapes=[
             pltpu.VMEM((rows, rows), f32),
             pltpu.VMEM((width, rows), f32),
@@ -254,10 +252,9 @@
             pltpu.SemaphoreType.DMA((SWEEPS - 1, 2, groups)),
             pltpu.SemaphoreType.DMA((3, n)),
             pltpu.SemaphoreType.DMA((3, n)),
-            pltpu.SemaphoreType.DMA((groups,)),
         ],
         compiler_params=pltpu.CompilerParams(
-            collective_id=0, has_side_effects=True),
+            collective_id=0, has_side_effects=True, vmem_limit_bytes=62 * 2**20),
     )(diag_blocks, lower_coupling.T, upper_coupling.T, right_sides)
 
 

time: 42.4 us -> 40.4 us (0.953)
  local copies, waits for them, and re-layouts: 2.88 us -> 1.58 us
  Pallas kernels: 38.7 us -> 38 us
    unnamed x4 -> x2, local copies, waits for them, and re-layouts: 2.88 us -> 1.58 us
    pallas_call x1, Pallas kernels: 38.7 us -> 38 us  [local(): pl.pallas_call(functools.partial(kernel, n), out_shape=(pltpu.VMEM((rows,...]
where the time goes in v3:
time: 40.4 us; the launch traced here: 40.2 us
  Pallas kernels  38 us (94%)
  local copies, waits for them, and re-layouts  1.58 us (4%)
  between operations  0.64 us (2%)
    pallas_call x1, Pallas kernels, local(): pl.pallas_call(functools.partial(kernel, n), out_shape=(pltpu.VMEM((rows,...  38 us
    unnamed x2, local copies, waits for them, and re-layouts  1.58 us

profile of v3, /device:TPU:0, one launch (start us, length us, event | category | flops | bytes accessed | tf_op | source)
XLA Modules:
  0.0 40.2 jit_solution(16305376595245394457)
XLA Ops:
  0.6 38.0 %shard_map.59 = (f32[512,512]{1,0:T(8,128)S(1)}, f32[8,512]{1,0:T(8,128)S(1)}) custom-call(f32[512,512]{1,0:T(8,128)} %d_hbm.1, f32[64,512]{1,0:T(8,128)} %bitcast.2, f32[64,512]{1,0:T(8,128)} %bitcast.3, f32[512,512]{1,0:T(8,128)} %b_hbm.1), custom_call_target="tpu_custom_call" | custom-call | tf_op jit(solution)/shard_map/pallas_call | solution.py:226
  38.7 1.0 %copy.8 = f32[512,512]{1,0:T(8,128)} copy(f32[512,512]{1,0:T(8,128)S(1)} %get-tuple-element.2) | data formatting | bytes 2097152
  39.6 0.6 %copy.9 = f32[8,512]{1,0:T(8,128)} copy(f32[8,512]{1,0:T(8,128)S(1)} %get-tuple-element.3) | data formatting | bytes 32768
